TPU v7x, 32 devices: a whole 2x2x4 slice. The times are simulated.
32 devices in a mesh: lat: 8 (over y, x, core), lon: 4 (over z).
Axes of the slice: x: 2, y: 2, z: 4, core: 2. Of those that a mesh axis runs over, the one named last changes fastest.
Arguments:
- inputs: bfloat16 [128, 384, 256], P('lat', 'lon'), may hold values from -6 to 6
- first_filter: bfloat16 [3, 3, 256, 256], replicated, may hold values from -0.125 to 0.125
- second_filter: bfloat16 [3, 3, 256, 256], replicated, may hold values from -0.125 to 0.125
- cotangent: bfloat16 [128, 384, 256], P('lat', 'lon'), may hold values from -30 to 30
Outputs:
- input_grad: bfloat16 [128, 384, 256], P('lat', 'lon')
- first_grad: float32 [3, 3, 256, 256], replicated
- second_grad: float32 [3, 3, 256, 256], replicated
All inputs are finite; a program needn't handle non-finite values.
Results may differ from a plain program's by a relative error of at most 0.0061.
Values may be sent and summed in bfloat16 or wider, within the bound.
A program may use at most 64 MiB of HBM per device.

v0:
```python
import jax
import jax.numpy as jnp
from jax import lax
from jax.sharding import PartitionSpec as P


def extended(block, sides, width):
    for axis, dim in sides:
        count = lax.axis_size(axis)
        forward = [(i, i + 1) for i in range(count - 1)]
        forward.append((count - 1, 0))
        backward = [(target, source) for source, target in forward]
        low = lax.ppermute(
            lax.slice_in_dim(block, block.shape[dim] - width, None, axis=dim), axis, forward
        )
        high = lax.ppermute(lax.slice_in_dim(block, 0, width, axis=dim), axis, backward)
        block = jnp.concatenate([low, block, high], axis=dim)
    return block


def mask_rows(padded, width):
    rows = padded.shape[0] - 2 * width
    position = lax.broadcasted_iota(jnp.int32, (padded.shape[0], 1, 1), 0)
    index = lax.axis_index("lat")
    count = lax.axis_size("lat")
    dropped = (position < width) & (index == 0) | (position >= rows + width) & (index == count - 1)
    return jnp.where(dropped, jnp.zeros((), padded.dtype), padded)


def extend(field):
    padded = extended(field, (("lat", 0), ("lon", 1)), 1)
    return mask_rows(padded, 1)


def conv_taps(padded, weight, rows, cols, flipped):
    total = jnp.zeros(
        (rows * cols, weight.shape[3] if not flipped else weight.shape[2]), jnp.float32
    )
    for first in range(3):
        for second in range(3):
            piece = padded[first : first + rows, second : second + cols, :].reshape(rows * cols, -1)
            if flipped:
                total = total + lax.dot_general(
                    piece,
                    weight[2 - first, 2 - second],
                    (((1,), (1,)), ((), ())),
                    preferred_element_type=jnp.float32,
                )
            else:
                total = total + jnp.dot(
                    piece, weight[first, second], preferred_element_type=jnp.float32
                )
    return total.reshape(rows, cols, -1)


def filter_grad(padded, delta, rows, cols):
    flat = delta.reshape(rows * cols, -1)
    taps = []
    for first in range(3):
        for second in range(3):
            piece = padded[first : first + rows, second : second + cols, :].reshape(rows * cols, -1)
            taps.append(
                lax.dot_general(
                    piece, flat, (((0,), (0,)), ((), ())), preferred_element_type=jnp.float32
                )
            )
    return jnp.stack(taps).reshape(3, 3, flat.shape[1], flat.shape[1])


def gelu_value(value):
    return value * 0.5 * (1.0 + jax.scipy.special.erf(value * 0.7071067811865476))


def gelu_slope(value):
    return (
        0.5 * (1.0 + jax.scipy.special.erf(value * 0.7071067811865476))
        + value * jnp.exp(-0.5 * value * value) * 0.3989422804014327
    )


def body(inputs, first_filter, second_filter, cotangent):
    rows, cols = (inputs.shape[0], inputs.shape[1])
    padded_in = extend(inputs)
    hidden_one = conv_taps(padded_in, first_filter, rows, cols, False)
    act = gelu_value(hidden_one).astype(jnp.bfloat16)
    padded_act = extend(act)
    hidden_two = conv_taps(padded_act, second_filter, rows, cols, False)
    delta_two = (cotangent.astype(jnp.float32) * gelu_slope(hidden_two)).astype(jnp.bfloat16)
    second_part = filter_grad(padded_act, delta_two, rows, cols)
    act_grad = conv_taps(extend(delta_two), second_filter, rows, cols, True)
    delta_one = (act_grad * gelu_slope(hidden_one)).astype(jnp.bfloat16)
    first_part = filter_grad(padded_in, delta_one, rows, cols)
    first_grad, second_grad = lax.psum((first_part, second_part), ("lat", "lon"))
    input_grad = conv_taps(extend(delta_one), first_filter, rows, cols, True).astype(jnp.bfloat16)
    return (input_grad, first_grad, second_grad)


def solution(mesh):
    in_specs = (P("lat", "lon", None), P(), P(), P("lat", "lon", None))
    out_specs = (P("lat", "lon", None), P(), P())
    return jax.shard_map(body, mesh=mesh, in_specs=in_specs, out_specs=out_specs, check_vma=False)
```

profile of v0, /device:TPU:0, one launch (start us, length us, event | category | flops | bytes accessed | tf_op | source)
XLA Modules:
  0.0 228.8 jit_solution(7460417335077282387)
XLA Ops:
  7.2 0.8 fusion.133
  8.6 2.9 %collective-permute-start.1 = (bf16[1,96,256]{2,1,0:T(8,128)(2,1)S(1)}, bf16[1,96,256]{2,1,0:T(8,128)(2,1)S(1)}, u32[]{:S(2)}, u32[]{:S(2)}) collective-permute-start(bf16[1,96,256]{2,1,0:T(8,128)(2,1)S(1)} %get-tuple-element.55), channel_id=1, source_target_pairs={{4,0},{8,4},{12,8},{16,12},{20,16},{24,20},{28,24},{0,28},{5,1},{9... | collective-permute-start | bytes 147464 | tf_op jit(solution)/shard_map/ppermute | solution.py:16
  11.5 1.7 collective-permute-done
  13.2 1.2 constant_dynamic-update-slice_fusion.1
  14.5 4.4 %collective-permute-start.3 = (bf16[18,1,256]{2,1,0:T(2,128)(2,1)S(1)}, bf16[18,1,256]{2,1,0:T(2,128)(2,1)S(1)}, u32[]{:S(2)}, u32[]{:S(2)}) collective-permute-start(bf16[18,1,256]{2,1,0:T(2,128)(2,1)S(1)} %get-tuple-element.48), channel_id=1, source_target_pairs={{1,0},{2,1},{3,2},{0,3},{5,4},{6,5},{7,6},{4,7},{9,8},{10,9},{11,1... | collective-permute-start | bytes 27656 | tf_op jit(solution)/shard_map/ppermute | solution.py:16
  18.9 1.5 collective-permute-done.3
  20.3 4.1 %collective-permute-done.2 = bf16[18,1,256]{2,1,0:T(2,128)(2,1)S(1)} collective-permute-done((bf16[18,1,256]{2,1,0:T(2,128)(2,1)S(1)}, bf16[18,1,256]{2,1,0:T(2,128)(2,1)S(1)}, u32[]{:S(2)}, u32[]{:S(2)}) %collective-permute-start.2) | collective-permute-done | bytes 9248 | tf_op jit(solution)/shard_map/ppermute | solution.py:13
  25.0 0.8 fusion.128
  30.5 1.4 collective-permute-done.5
  31.9 2.6 %collective-permute-done.4 = bf16[1,96,256]{2,1,0:T(8,128)(2,1)S(1)} collective-permute-done((bf16[1,96,256]{2,1,0:T(8,128)(2,1)S(1)}, bf16[1,96,256]{2,1,0:T(8,128)(2,1)S(1)}, u32[]{:S(2)}, u32[]{:S(2)}) %collective-permute-start.4) | collective-permute-done | bytes 49184 | tf_op jit(solution)/shard_map/ppermute | solution.py:13
  34.8 1.8 collective-permute-start.6
  36.6 1.7 collective-permute-done.7
  38.4 2.0 collective-permute-done.6
  40.9 1.1 fusion.127
  45.5 0.7 copy-done.5
  46.3 0.7 fusion.6
  51.0 1.1 collective-permute-done.8
  52.2 2.0 collective-permute-start.10
  54.7 1.3 collective-permute-done.11
  56.0 1.9 collective-permute-done.10
  58.4 1.1 fusion.126
  63.1 0.7 fusion.12
  64.2 0.6 collective-permute-start.13
  67.8 1.4 collective-permute-done.12
  69.3 2.0 collective-permute-start.14
  71.8 1.4 copy-done.4
  73.2 2.0 collective-permute-done.14
  75.7 1.1 fusion.125
  80.1 1.3 fusion
  81.4 135.8 %all-reduce.3.cloned.1.call-done = (f32[3,3,256,256]{3,2,1,0:T(8,128)}, f32[3,3,256,256]{3,2,1,0:T(8,128)}) async-done(((f32[3,3,256,256]{3,2,1,0:T(8,128)}, f32[3,3,256,256]{3,2,1,0:T(8,128)}), (f32[3,3,256,256]{3,2,1,0:T(8,128)}, f32[3,3,256,256]{3,2,1,0:T(8,128)})) %all-reduce.3.cloned.1.call-update) | async-done | bytes 4718608 | tf_op jit(solution)/shard_map/psum | solution.py:93
  217.2 3.4 %copy.27 = f32[3,3,256,256]{3,2,1,0:T(8,128)} copy(f32[3,3,256,256]{3,2,1,0:T(8,128)} %get-tuple-element.58) | data formatting | bytes 4718592
  220.5 1.4 copy.28
  (94 shorter events, 26.5 us)
Async XLA Ops:
  7.2 210.0 %all-reduce.3.cloned.1.call-start = ((), (), s32[]{:S(2)}) async-start(), calls=%async_computation | async-start | bytes 9437184 | tf_op jit(solution)/shard_map/psum | solution.py:93
  8.0 5.2 %collective-permute-start = (bf16[1,96,256]{2,1,0:T(8,128)(2,1)S(1)}, bf16[1,96,256]{2,1,0:T(8,128)(2,1)S(1)}, u32[]{:S(2)}, u32[]{:S(2)}) collective-permute-start(bf16[1,96,256]{2,1,0:T(8,128)(2,1)S(1)} %get-tuple-element.56), channel_id=1, source_target_pairs={{0,4},{4,8},{8,12},{12,16},{16,20},{20,24},{24,28},{28,0},{1,5},{5... | collective-permute-start | bytes 147464 | tf_op jit(solution)/shard_map/ppermute | solution.py:13
  8.6 5.8 %collective-permute-start.1 = (bf16[1,96,256]{2,1,0:T(8,128)(2,1)S(1)}, bf16[1,96,256]{2,1,0:T(8,128)(2,1)S(1)}, u32[]{:S(2)}, u32[]{:S(2)}) collective-permute-start(bf16[1,96,256]{2,1,0:T(8,128)(2,1)S(1)} %get-tuple-element.55), channel_id=1, source_target_pairs={{4,0},{8,4},{12,8},{16,12},{20,16},{24,20},{28,24},{0,28},{5,1},{9... | collective-permute-start | bytes 147464 | tf_op jit(solution)/shard_map/ppermute | solution.py:16
  14.5 5.9 %collective-permute-start.3 = (bf16[18,1,256]{2,1,0:T(2,128)(2,1)S(1)}, bf16[18,1,256]{2,1,0:T(2,128)(2,1)S(1)}, u32[]{:S(2)}, u32[]{:S(2)}) collective-permute-start(bf16[18,1,256]{2,1,0:T(2,128)(2,1)S(1)} %get-tuple-element.48), channel_id=1, source_target_pairs={{1,0},{2,1},{3,2},{0,3},{5,4},{6,5},{7,6},{4,7},{9,8},{10,9},{11,1... | collective-permute-start | bytes 27656 | tf_op jit(solution)/shard_map/ppermute | solution.py:16
  18.9 5.6 %collective-permute-start.2 = (bf16[18,1,256]{2,1,0:T(2,128)(2,1)S(1)}, bf16[18,1,256]{2,1,0:T(2,128)(2,1)S(1)}, u32[]{:S(2)}, u32[]{:S(2)}) collective-permute-start(bf16[18,1,256]{2,1,0:T(2,128)(2,1)S(1)} %get-tuple-element.47), channel_id=1, source_target_pairs={{0,1},{1,2},{2,3},{3,0},{4,5},{5,6},{6,7},{7,4},{8,9},{9,10},{10,1... | collective-permute-start | bytes 27656 | tf_op jit(solution)/shard_map/ppermute | solution.py:13
  25.0 1.3 copy-start.1
  30.0 2.0 collective-permute-start.5
  30.0 4.5 %collective-permute-start.4 = (bf16[1,96,256]{2,1,0:T(8,128)(2,1)S(1)}, bf16[1,96,256]{2,1,0:T(8,128)(2,1)S(1)}, u32[]{:S(2)}, u32[]{:S(2)}) collective-permute-start(bf16[1,96,256]{2,1,0:T(8,128)(2,1)S(1)} %get-tuple-element.53), channel_id=1, source_target_pairs={{0,4},{4,8},{8,12},{12,16},{16,20},{20,24},{24,28},{28,0},{1,5},{5... | collective-permute-start | bytes 147464 | tf_op jit(solution)/shard_map/ppermute | solution.py:13
  34.5 3.8 %collective-permute-start.7 = (bf16[18,1,256]{2,1,0:T(2,128)(2,1)S(1)}, bf16[18,1,256]{2,1,0:T(2,128)(2,1)S(1)}, u32[]{:S(2)}, u32[]{:S(2)}) collective-permute-start(bf16[18,1,256]{2,1,0:T(2,128)(2,1)S(1)} %get-tuple-element.46), channel_id=1, source_target_pairs={{1,0},{2,1},{3,2},{0,3},{5,4},{6,5},{7,6},{4,7},{9,8},{10,9},{11,1... | collective-permute-start | bytes 27656 | tf_op jit(solution)/shard_map/ppermute | solution.py:16
  34.8 5.6 %collective-permute-start.6 = (bf16[18,1,256]{2,1,0:T(2,128)(2,1)S(1)}, bf16[18,1,256]{2,1,0:T(2,128)(2,1)S(1)}, u32[]{:S(2)}, u32[]{:S(2)}) collective-permute-start(bf16[18,1,256]{2,1,0:T(2,128)(2,1)S(1)} %get-tuple-element.45), channel_id=1, source_target_pairs={{0,1},{1,2},{2,3},{3,0},{4,5},{5,6},{6,7},{7,4},{8,9},{9,10},{10,1... | collective-permute-start | bytes 27656 | tf_op jit(solution)/shard_map/ppermute | solution.py:13
  40.9 1.3 copy-start
  45.1 1.1 copy-start.5
  47.4 3.6 %collective-permute-start.9 = (bf16[1,96,256]{2,1,0:T(8,128)(2,1)S(1)}, bf16[1,96,256]{2,1,0:T(8,128)(2,1)S(1)}, u32[]{:S(2)}, u32[]{:S(2)}) collective-permute-start(bf16[1,96,256]{2,1,0:T(8,128)(2,1)S(1)} %get-tuple-element.52), channel_id=1, source_target_pairs={{4,0},{8,4},{12,8},{16,12},{20,16},{24,20},{28,24},{0,28},{5,1},{9... | collective-permute-start | bytes 147464 | tf_op jit(solution)/shard_map/ppermute | solution.py:16
  47.5 4.6 %collective-permute-start.8 = (bf16[1,96,256]{2,1,0:T(8,128)(2,1)S(1)}, bf16[1,96,256]{2,1,0:T(8,128)(2,1)S(1)}, u32[]{:S(2)}, u32[]{:S(2)}) collective-permute-start(bf16[1,96,256]{2,1,0:T(8,128)(2,1)S(1)} %get-tuple-element.51), channel_id=1, source_target_pairs={{0,4},{4,8},{8,12},{12,16},{16,20},{20,24},{24,28},{28,0},{1,5},{5... | collective-permute-start | bytes 147464 | tf_op jit(solution)/shard_map/ppermute | solution.py:13
  52.2 3.8 %collective-permute-start.11 = (bf16[18,1,256]{2,1,0:T(2,128)(2,1)S(1)}, bf16[18,1,256]{2,1,0:T(2,128)(2,1)S(1)}, u32[]{:S(2)}, u32[]{:S(2)}) collective-permute-start(bf16[18,1,256]{2,1,0:T(2,128)(2,1)S(1)} %get-tuple-element.44), channel_id=1, source_target_pairs={{1,0},{2,1},{3,2},{0,3},{5,4},{6,5},{7,6},{4,7},{9,8},{10,9},{11,1... | collective-permute-start | bytes 27656 | tf_op jit(solution)/shard_map/ppermute | solution.py:16
  52.2 5.6 %collective-permute-start.10 = (bf16[18,1,256]{2,1,0:T(2,128)(2,1)S(1)}, bf16[18,1,256]{2,1,0:T(2,128)(2,1)S(1)}, u32[]{:S(2)}, u32[]{:S(2)}) collective-permute-start(bf16[18,1,256]{2,1,0:T(2,128)(2,1)S(1)} %get-tuple-element.43), channel_id=1, source_target_pairs={{0,1},{1,2},{2,3},{3,0},{4,5},{5,6},{6,7},{7,4},{8,9},{9,10},{10,1... | collective-permute-start | bytes 27656 | tf_op jit(solution)/shard_map/ppermute | solution.py:13
  54.7 4.8 %copy-start.3 = (f32[9,256,256]{2,1,0:T(8,128)}, f32[9,256,256]{2,1,0:T(8,128)S(1)}, u32[]{:S(2)}) copy-start(f32[9,256,256]{2,1,0:T(8,128)S(1)} %fusion.13) | copy-start | bytes 7077892
  64.2 3.6 %collective-permute-start.13 = (bf16[1,96,256]{2,1,0:T(8,128)(2,1)S(1)}, bf16[1,96,256]{2,1,0:T(8,128)(2,1)S(1)}, u32[]{:S(2)}, u32[]{:S(2)}) collective-permute-start(bf16[1,96,256]{2,1,0:T(8,128)(2,1)S(1)} %get-tuple-element.50), channel_id=1, source_target_pairs={{4,0},{8,4},{12,8},{16,12},{20,16},{24,20},{28,24},{0,28},{5,1},{9... | collective-permute-start | bytes 147464 | tf_op jit(solution)/shard_map/ppermute | solution.py:16
  64.8 4.4 %collective-permute-start.12 = (bf16[1,96,256]{2,1,0:T(8,128)(2,1)S(1)}, bf16[1,96,256]{2,1,0:T(8,128)(2,1)S(1)}, u32[]{:S(2)}, u32[]{:S(2)}) collective-permute-start(bf16[1,96,256]{2,1,0:T(8,128)(2,1)S(1)} %get-tuple-element.49), channel_id=1, source_target_pairs={{0,4},{4,8},{8,12},{12,16},{16,20},{20,24},{24,28},{28,0},{1,5},{5... | collective-permute-start | bytes 147464 | tf_op jit(solution)/shard_map/ppermute | solution.py:13
  69.2 3.9 %collective-permute-start.15 = (bf16[18,1,256]{2,1,0:T(2,128)(2,1)S(1)}, bf16[18,1,256]{2,1,0:T(2,128)(2,1)S(1)}, u32[]{:S(2)}, u32[]{:S(2)}) collective-permute-start(bf16[18,1,256]{2,1,0:T(2,128)(2,1)S(1)} %get-tuple-element.42), channel_id=1, source_target_pairs={{1,0},{2,1},{3,2},{0,3},{5,4},{6,5},{7,6},{4,7},{9,8},{10,9},{11,1... | collective-permute-start | bytes 27656 | tf_op jit(solution)/shard_map/ppermute | solution.py:16
  69.3 5.8 %collective-permute-start.14 = (bf16[18,1,256]{2,1,0:T(2,128)(2,1)S(1)}, bf16[18,1,256]{2,1,0:T(2,128)(2,1)S(1)}, u32[]{:S(2)}, u32[]{:S(2)}) collective-permute-start(bf16[18,1,256]{2,1,0:T(2,128)(2,1)S(1)} %get-tuple-element.41), channel_id=1, source_target_pairs={{0,1},{1,2},{2,3},{3,0},{4,5},{5,6},{6,7},{7,4},{8,9},{9,10},{10,1... | collective-permute-start | bytes 27656 | tf_op jit(solution)/shard_map/ppermute | solution.py:13
  71.7 1.4 copy-start.4
  217.2 3.4 %copy-start.2 = (f32[3,3,256,256]{3,2,1,0:T(8,128)S(1)}, f32[3,3,256,256]{3,2,1,0:T(8,128)}, u32[]{:S(2)}) copy-start(f32[3,3,256,256]{3,2,1,0:T(8,128)} %get-tuple-element.59) | copy-start | bytes 7077892
Sparse Core Ops, SparseCore 0:
  73.3 143.8 all-reduce.2
where the time goes:
time: 229 us
  waiting for transfers between devices  158 us (69%)
  matrix products  22.3 us (10%)
  starting transfers between devices  15.8 us (7%)
  between operations  14.6 us (6%)
  local copies, waits for them, and re-layouts  13.6 us (6%)
  other arithmetic  4.03 us (2%)
    psum x1, waiting for transfers between devices, body(): lax.psum((first_part, second_part), ('lat', 'lon'))  136 us
    ppermute x8, waiting for transfers between devices, extended(): lax.ppermute(lax.slice_in_dim(block, block.shape[dim] - width, None, axis...  16.7 us
    unnamed x16, local copies, waits for them, and re-layouts  8.77 us
    ppermute x8, starting transfers between devices, extended(): lax.ppermute(lax.slice_in_dim(block, 0, width, axis=dim), axis, backward)  8.4 us
    dot_general x18, matrix products, conv_taps(): lax.dot_general(piece, weight[2 - first, 2 - second], (((1,), (1,)), ((),...  8.18 us
    dot_general x18, matrix products, filter_grad(): lax.dot_general(piece, flat, (((0,), (0,)), ((), ())), preferred_element_...  7.54 us
    ppermute x8, starting transfers between devices, extended(): lax.ppermute(lax.slice_in_dim(block, block.shape[dim] - width, None, axis...  7.38 us
    dot_general x18, matrix products, conv_taps(): jnp.dot(piece, weight[first, second], preferred_element_type=jnp.float32)  6.59 us
  transfers between devices with their start and end apart: 17, of which 13 were waited for; matrix products, arithmetic and copies ran while one was open for 6% of the time, Pallas kernels for 0%

commit v1 on v0

--- a/solution.py
+++ b/solution.py
@@ -90,7 +90,7 @@
     act_grad = conv_taps(extend(delta_two), second_filter, rows, cols, True)
     delta_one = (act_grad * gelu_slope(hidden_one)).astype(jnp.bfloat16)
     first_part = filter_grad(padded_in, delta_one, rows, cols)
-    first_grad, second_grad = lax.psum((first_part, second_part), ("lat", "lon"))
+    first_grad, second_grad = lax.psum(lax.psum((first_part, second_part), "lon"), "lat")
     input_grad = conv_taps(extend(delta_one), first_filter, rows, cols, True).astype(jnp.bfloat16)
     return (input_grad, first_grad, second_grad)
 

time: 229 us -> 341 us (1.49)
  waiting for transfers between devices: 158 us -> 263 us
  local copies, waits for them, and re-layouts: 13.6 us -> 19.3 us
    psum x1 -> x2, waiting for transfers between devices: 136 us -> 235 us  [the longest x1 155 us: body(): lax.psum((first_part, second_part), 'lon')]
    ppermute x8, waiting for transfers between devices: 5.89 us -> 9.86 us  [extended(): lax.ppermute(lax.slice_in_dim(block, 0, width, axis=dim), axis, backward)]
    unnamed x16 -> x28, local copies, waits for them, and re-layouts: 8.77 us -> 12.2 us
  transfers between devices with their start and end apart: 17 -> 18, of which waited for: 13 -> 16; matrix products, arithmetic and copies ran while one was open for 6% -> 4% of each run, Pallas kernels for 0% -> 0%
where the time goes in v1:
time: 341 us; the launch traced here: 340 us
  waiting for transfers between devices  263 us (77%)
  matrix products  23.5 us (7%)
  local copies, waits for them, and re-layouts  19.3 us (6%)
  starting transfers between devices  15.9 us (5%)
  between operations  14.6 us (4%)
  other arithmetic  4.07 us (1%)
    psum x1, waiting for transfers between devices, body(): lax.psum((first_part, second_part), 'lon')  155 us
    psum x1, waiting for transfers between devices, body(): lax.psum(lax.psum((first_part, second_part), 'lon'), 'lat')  80 us
    ppermute x8, waiting for transfers between devices, extended(): lax.ppermute(lax.slice_in_dim(block, block.shape[dim] - width, None, axis...  18 us
    unnamed x28, local copies, waits for them, and re-layouts  12.2 us
    ppermute x8, waiting for transfers between devices, extended(): lax.ppermute(lax.slice_in_dim(block, 0, width, axis=dim), axis, backward)  9.86 us
    dot_general x18, matrix products, conv_taps(): lax.dot_general(piece, weight[2 - first, 2 - second], (((1,), (1,)), ((),...  9.24 us
    ppermute x8, starting transfers between devices, extended(): lax.ppermute(lax.slice_in_dim(block, 0, width, axis=dim), axis, backward)  8.35 us
    dot_general x18, matrix products, filter_grad(): lax.dot_general(piece, flat, (((0,), (0,)), ((), ())), preferred_element_...  7.53 us
  transfers between devices with their start and end apart: 18, of which 16 were waited for; matrix products, arithmetic and copies ran while one was open for 4% of the time, Pallas kernels for 0%

profile of v1, /device:TPU:0, one launch (start us, length us, event | category | flops | bytes accessed | tf_op | source)
XLA Modules:
  0.0 339.9 jit_solution(12427262720204764210)
XLA Ops:
  7.2 0.8 fusion.133
  8.6 2.9 collective-permute-start.1
  11.5 1.7 collective-permute-done
  13.2 1.2 constant_dynamic-update-slice_fusion.1
  14.5 4.4 %collective-permute-start.3 = (bf16[18,1,256]{2,1,0:T(2,128)(2,1)S(1)}, bf16[18,1,256]{2,1,0:T(2,128)(2,1)S(1)}, u32[]{:S(2)}, u32[]{:S(2)}) collective-permute-start(bf16[18,1,256]{2,1,0:T(2,128)(2,1)S(1)} %get-tuple-element.50), channel_id=1, source_target_pairs={{1,0},{2,1},{3,2},{0,3},{5,4},{6,5},{7,6},{4,7},{9,8},{10,9},{11,1... | collective-permute-start | bytes 27656 | tf_op jit(solution)/shard_map/ppermute | solution.py:16
  18.9 1.5 collective-permute-done.3
  20.3 4.1 %collective-permute-done.2 = bf16[18,1,256]{2,1,0:T(2,128)(2,1)S(1)} collective-permute-done((bf16[18,1,256]{2,1,0:T(2,128)(2,1)S(1)}, bf16[18,1,256]{2,1,0:T(2,128)(2,1)S(1)}, u32[]{:S(2)}, u32[]{:S(2)}) %collective-permute-start.2) | collective-permute-done | bytes 9248 | tf_op jit(solution)/shard_map/ppermute | solution.py:13
  25.0 1.1 fusion.128
  30.6 1.4 collective-permute-done.5
  32.1 2.6 collective-permute-done.4
  34.8 1.9 collective-permute-start.6
  36.7 1.7 collective-permute-done.7
  38.5 1.9 collective-permute-done.6
  41.0 1.1 fusion.127
  51.1 1.1 collective-permute-done.8
  52.3 2.0 collective-permute-start.10
  54.8 1.3 collective-permute-done.11
  56.1 1.9 collective-permute-done.10
  58.5 1.0 fusion.126
  67.6 1.4 copy-done.10
  69.7 1.7 collective-permute-done.13
  71.4 2.7 collective-permute-done.12
  74.2 2.0 collective-permute-start.14
  76.2 2.3 collective-permute-done.15
  78.4 2.1 collective-permute-done.14
  81.1 3.1 fusion.125
  84.6 154.7 %all-reduce.7.cloned.1.call-done = (f32[3,3,256,256]{3,2,1,0:T(8,128)}, f32[3,3,256,256]{3,2,1,0:T(8,128)}) async-done(((f32[3,3,256,256]{3,2,1,0:T(8,128)}, f32[3,3,256,256]{3,2,1,0:T(8,128)}), (f32[3,3,256,256]{3,2,1,0:T(8,128)}, f32[3,3,256,256]{3,2,1,0:T(8,128)})) %all-reduce.7.cloned.1.call-update) | async-done | bytes 4718608 | tf_op jit(solution)/shard_map/psum | solution.py:93
  239.4 1.6 convolution_add_fusion.7
  247.1 1.3 fusion
  248.4 80.0 %all-reduce.5.cloned.1.call-done = (f32[3,3,256,256]{3,2,1,0:T(8,128)}, f32[3,3,256,256]{3,2,1,0:T(8,128)}) async-done(((f32[3,3,256,256]{3,2,1,0:T(8,128)}, f32[3,3,256,256]{3,2,1,0:T(8,128)}), (f32[3,3,256,256]{3,2,1,0:T(8,128)}, f32[3,3,256,256]{3,2,1,0:T(8,128)})) %all-reduce.5.cloned.1.call-update) | async-done | bytes 4718608 | tf_op jit(solution)/shard_map/psum | solution.py:93
  328.3 3.4 copy.29
  331.7 1.4 copy.30
  (109 shorter events, 32.2 us)
Async XLA Ops:
  7.2 232.2 %all-reduce.7.cloned.1.call-start = ((), (), s32[]{:S(2)}) async-start(), calls=%async_computation.1 | async-start | bytes 9437184 | tf_op jit(solution)/shard_map/psum | solution.py:93
  8.0 5.2 %collective-permute-start = (bf16[1,96,256]{2,1,0:T(8,128)(2,1)S(1)}, bf16[1,96,256]{2,1,0:T(8,128)(2,1)S(1)}, u32[]{:S(2)}, u32[]{:S(2)}) collective-permute-start(bf16[1,96,256]{2,1,0:T(8,128)(2,1)S(1)} %get-tuple-element.58), channel_id=1, source_target_pairs={{0,4},{4,8},{8,12},{12,16},{16,20},{20,24},{24,28},{28,0},{1,5},{5... | collective-permute-start | bytes 147464 | tf_op jit(solution)/shard_map/ppermute | solution.py:13
  8.6 5.8 %collective-permute-start.1 = (bf16[1,96,256]{2,1,0:T(8,128)(2,1)S(1)}, bf16[1,96,256]{2,1,0:T(8,128)(2,1)S(1)}, u32[]{:S(2)}, u32[]{:S(2)}) collective-permute-start(bf16[1,96,256]{2,1,0:T(8,128)(2,1)S(1)} %get-tuple-element.57), channel_id=1, source_target_pairs={{4,0},{8,4},{12,8},{16,12},{20,16},{24,20},{28,24},{0,28},{5,1},{9... | collective-permute-start | bytes 147464 | tf_op jit(solution)/shard_map/ppermute | solution.py:16
  14.5 5.9 %collective-permute-start.3 = (bf16[18,1,256]{2,1,0:T(2,128)(2,1)S(1)}, bf16[18,1,256]{2,1,0:T(2,128)(2,1)S(1)}, u32[]{:S(2)}, u32[]{:S(2)}) collective-permute-start(bf16[18,1,256]{2,1,0:T(2,128)(2,1)S(1)} %get-tuple-element.50), channel_id=1, source_target_pairs={{1,0},{2,1},{3,2},{0,3},{5,4},{6,5},{7,6},{4,7},{9,8},{10,9},{11,1... | collective-permute-start | bytes 27656 | tf_op jit(solution)/shard_map/ppermute | solution.py:16
  18.9 5.6 %collective-permute-start.2 = (bf16[18,1,256]{2,1,0:T(2,128)(2,1)S(1)}, bf16[18,1,256]{2,1,0:T(2,128)(2,1)S(1)}, u32[]{:S(2)}, u32[]{:S(2)}) collective-permute-start(bf16[18,1,256]{2,1,0:T(2,128)(2,1)S(1)} %get-tuple-element.49), channel_id=1, source_target_pairs={{0,1},{1,2},{2,3},{3,0},{4,5},{5,6},{6,7},{7,4},{8,9},{9,10},{10,1... | collective-permute-start | bytes 27656 | tf_op jit(solution)/shard_map/ppermute | solution.py:13
  25.0 1.3 copy-start.1
  30.1 2.0 collective-permute-start.5
  30.1 4.5 %collective-permute-start.4 = (bf16[1,96,256]{2,1,0:T(8,128)(2,1)S(1)}, bf16[1,96,256]{2,1,0:T(8,128)(2,1)S(1)}, u32[]{:S(2)}, u32[]{:S(2)}) collective-permute-start(bf16[1,96,256]{2,1,0:T(8,128)(2,1)S(1)} %get-tuple-element.55), channel_id=1, source_target_pairs={{0,4},{4,8},{8,12},{12,16},{16,20},{20,24},{24,28},{28,0},{1,5},{5... | collective-permute-start | bytes 147464 | tf_op jit(solution)/shard_map/ppermute | solution.py:13
  34.6 3.8 %collective-permute-start.7 = (bf16[18,1,256]{2,1,0:T(2,128)(2,1)S(1)}, bf16[18,1,256]{2,1,0:T(2,128)(2,1)S(1)}, u32[]{:S(2)}, u32[]{:S(2)}) collective-permute-start(bf16[18,1,256]{2,1,0:T(2,128)(2,1)S(1)} %get-tuple-element.48), channel_id=1, source_target_pairs={{1,0},{2,1},{3,2},{0,3},{5,4},{6,5},{7,6},{4,7},{9,8},{10,9},{11,1... | collective-permute-start | bytes 27656 | tf_op jit(solution)/shard_map/ppermute | solution.py:16
  34.8 5.6 %collective-permute-start.6 = (bf16[18,1,256]{2,1,0:T(2,128)(2,1)S(1)}, bf16[18,1,256]{2,1,0:T(2,128)(2,1)S(1)}, u32[]{:S(2)}, u32[]{:S(2)}) collective-permute-start(bf16[18,1,256]{2,1,0:T(2,128)(2,1)S(1)} %get-tuple-element.47), channel_id=1, source_target_pairs={{0,1},{1,2},{2,3},{3,0},{4,5},{5,6},{6,7},{7,4},{8,9},{9,10},{10,1... | collective-permute-start | bytes 27656 | tf_op jit(solution)/shard_map/ppermute | solution.py:13
  41.0 1.3 copy-start
  45.2 1.1 copy-start.11
  47.5 3.6 %collective-permute-start.9 = (bf16[1,96,256]{2,1,0:T(8,128)(2,1)S(1)}, bf16[1,96,256]{2,1,0:T(8,128)(2,1)S(1)}, u32[]{:S(2)}, u32[]{:S(2)}) collective-permute-start(bf16[1,96,256]{2,1,0:T(8,128)(2,1)S(1)} %get-tuple-element.54), channel_id=1, source_target_pairs={{4,0},{8,4},{12,8},{16,12},{20,16},{24,20},{28,24},{0,28},{5,1},{9... | collective-permute-start | bytes 147464 | tf_op jit(solution)/shard_map/ppermute | solution.py:16
  47.6 4.6 %collective-permute-start.8 = (bf16[1,96,256]{2,1,0:T(8,128)(2,1)S(1)}, bf16[1,96,256]{2,1,0:T(8,128)(2,1)S(1)}, u32[]{:S(2)}, u32[]{:S(2)}) collective-permute-start(bf16[1,96,256]{2,1,0:T(8,128)(2,1)S(1)} %get-tuple-element.53), channel_id=1, source_target_pairs={{0,4},{4,8},{8,12},{12,16},{16,20},{20,24},{24,28},{28,0},{1,5},{5... | collective-permute-start | bytes 147464 | tf_op jit(solution)/shard_map/ppermute | solution.py:13
  52.2 3.8 %collective-permute-start.11 = (bf16[18,1,256]{2,1,0:T(2,128)(2,1)S(1)}, bf16[18,1,256]{2,1,0:T(2,128)(2,1)S(1)}, u32[]{:S(2)}, u32[]{:S(2)}) collective-permute-start(bf16[18,1,256]{2,1,0:T(2,128)(2,1)S(1)} %get-tuple-element.46), channel_id=1, source_target_pairs={{1,0},{2,1},{3,2},{0,3},{5,4},{6,5},{7,6},{4,7},{9,8},{10,9},{11,1... | collective-permute-start | bytes 27656 | tf_op jit(solution)/shard_map/ppermute | solution.py:16
  52.3 5.6 %collective-permute-start.10 = (bf16[18,1,256]{2,1,0:T(2,128)(2,1)S(1)}, bf16[18,1,256]{2,1,0:T(2,128)(2,1)S(1)}, u32[]{:S(2)}, u32[]{:S(2)}) collective-permute-start(bf16[18,1,256]{2,1,0:T(2,128)(2,1)S(1)} %get-tuple-element.45), channel_id=1, source_target_pairs={{0,1},{1,2},{2,3},{3,0},{4,5},{5,6},{6,7},{7,4},{8,9},{9,10},{10,1... | collective-permute-start | bytes 27656 | tf_op jit(solution)/shard_map/ppermute | solution.py:13
  54.8 4.7 %copy-start.9 = (f32[9,256,256]{2,1,0:T(8,128)}, f32[9,256,256]{2,1,0:T(8,128)S(1)}, u32[]{:S(2)}) copy-start(f32[9,256,256]{2,1,0:T(8,128)S(1)} %fusion.13) | copy-start | bytes 7077892
  67.6 1.4 copy-start.10
  69.0 259.3 %all-reduce.5.cloned.1.call-start = ((), (), s32[]{:S(2)}) async-start(), calls=%async_computation | async-start | bytes 9437184 | tf_op jit(solution)/shard_map/psum | solution.py:93
  69.1 2.3 collective-permute-start.13
  69.6 4.4 %collective-permute-start.12 = (bf16[1,96,256]{2,1,0:T(8,128)(2,1)S(1)}, bf16[1,96,256]{2,1,0:T(8,128)(2,1)S(1)}, u32[]{:S(2)}, u32[]{:S(2)}) collective-permute-start(bf16[1,96,256]{2,1,0:T(8,128)(2,1)S(1)} %get-tuple-element.51), channel_id=1, source_target_pairs={{0,4},{4,8},{8,12},{12,16},{16,20},{20,24},{24,28},{28,0},{1,5},{5... | collective-permute-start | bytes 147464 | tf_op jit(solution)/shard_map/ppermute | solution.py:13
  74.1 4.3 %collective-permute-start.15 = (bf16[18,1,256]{2,1,0:T(2,128)(2,1)S(1)}, bf16[18,1,256]{2,1,0:T(2,128)(2,1)S(1)}, u32[]{:S(2)}, u32[]{:S(2)}) collective-permute-start(bf16[18,1,256]{2,1,0:T(2,128)(2,1)S(1)} %get-tuple-element.44), channel_id=1, source_target_pairs={{1,0},{2,1},{3,2},{0,3},{5,4},{6,5},{7,6},{4,7},{9,8},{10,9},{11,1... | collective-permute-start | bytes 27656 | tf_op jit(solution)/shard_map/ppermute | solution.py:16
  74.2 6.3 %collective-permute-start.14 = (bf16[18,1,256]{2,1,0:T(2,128)(2,1)S(1)}, bf16[18,1,256]{2,1,0:T(2,128)(2,1)S(1)}, u32[]{:S(2)}, u32[]{:S(2)}) collective-permute-start(bf16[18,1,256]{2,1,0:T(2,128)(2,1)S(1)} %get-tuple-element.43), channel_id=1, source_target_pairs={{0,1},{1,2},{2,3},{3,0},{4,5},{5,6},{6,7},{7,4},{8,9},{9,10},{10,1... | collective-permute-start | bytes 27656 | tf_op jit(solution)/shard_map/ppermute | solution.py:13
  239.4 1.6 copy-start.7
  241.0 1.1 copy-start.6
  242.2 1.1 copy-start.5
  243.3 1.1 copy-start.4
  244.4 1.1 copy-start.3
  245.6 1.1 copy-start.2
  328.3 3.4 copy-start.8
Sparse Core Ops, SparseCore 0:
  69.2 170.1 all-reduce.6
  242.7 85.5 all-reduce.4
